TPU v7x, 32 devices: a whole 2x2x4 slice. The times are simulated.
32 devices in a mesh: dp: 8 (over z, y), tensor: 4 (over x, core).
Axes of the slice: x: 2, y: 2, z: 4, core: 2. Of those that a mesh axis runs over, the one named last changes fastest.
Arguments:
- tokens: bfloat16 [8192, 2048], P(('dp', 'tensor')), may hold values from -6 to 6
- lengths: int32 [8], P('dp'), may hold values from 256 to 1024, as said below
- ln1_gain: float32 [2048], replicated, may hold values from 0.5 to 1.5
- ln1_bias: float32 [2048], replicated, may hold values from -3 to 3
- w_query: bfloat16 [2048, 2048], P(None, 'tensor'), may hold values from -0.125 to 0.125
- w_key: bfloat16 [2048, 2048], P(None, 'tensor'), may hold values from -0.125 to 0.125
- w_value: bfloat16 [2048, 4096], P(None, 'tensor'), may hold values from -0.125 to 0.125
- w_gate: bfloat16 [2048, 4096], P(None, 'tensor'), may hold values from -0.125 to 0.125
- w_out: bfloat16 [4096, 2048], P('tensor'), may hold values from -0.1875 to 0.1875
- ln2_gain: float32 [2048], replicated, may hold values from 0.5 to 1.5
- ln2_bias: float32 [2048], replicated, may hold values from -3 to 3
- mlp_gate: bfloat16 [2048, 4096], P(None, 'tensor'), may hold values from -0.125 to 0.125
- mlp_up: bfloat16 [2048, 4096], P(None, 'tensor'), may hold values from -0.125 to 0.125
- mlp_down: bfloat16 [4096, 2048], P('tensor'), may hold values from -0.1875 to 0.1875
- cotangent: bfloat16 [8192, 2048], P(('dp', 'tensor')), may hold values from -6 to 6
Outputs:
- mixed: bfloat16 [8192, 2048], P(('dp', 'tensor'))
- grad_tokens: float32 [8192, 2048], P(('dp', 'tensor'))
- grad_ln1_gain: float32 [2048], P(('dp', 'tensor'))
- grad_ln1_bias: float32 [2048], P(('dp', 'tensor'))
- grad_w_query: float32 [2048, 2048], P('dp', 'tensor')
- grad_w_key: float32 [2048, 2048], P('dp', 'tensor')
- grad_w_value: float32 [2048, 4096], P('dp', 'tensor')
- grad_w_gate: float32 [2048, 4096], P('dp', 'tensor')
- grad_w_out: float32 [4096, 2048], P('tensor', 'dp')
- grad_ln2_gain: float32 [2048], P(('dp', 'tensor'))
- grad_ln2_bias: float32 [2048], P(('dp', 'tensor'))
- grad_mlp_gate: float32 [2048, 4096], P('dp', 'tensor')
- grad_mlp_up: float32 [2048, 4096], P('dp', 'tensor')
- grad_mlp_down: float32 [4096, 2048], P('tensor', 'dp')
Inputs may be any that keep to these rules, and one draw needn't show every extreme that they name: Slot s holds one sequence in its first lengths[s] positions, the rest is padding; in every draw some slot is full (1024 tokens).
All inputs are finite; a program needn't handle non-finite values.
Results may differ from a plain program's by a relative error of at most 0.028.
Values may be sent and summed in bfloat16 or wider, within the bound.
A program may use at most 256 MiB of HBM per device.

v0:
```python
import jax
import jax.numpy as jnp
from jax import lax
from jax.sharding import PartitionSpec as P

KEY_HEAD = 256
VAL_HEAD = 512
SEQ = 1024
epsilon = 1e-05
three_pass = lax.Precision.HIGH


def norm_rows(values, gain_in, bias_in):
    centre = values - jnp.mean(values, axis=-1, keepdims=True)
    spread = jnp.mean(centre * centre, axis=-1, keepdims=True)
    return centre * lax.rsqrt(spread + epsilon) * gain_in + bias_in


def gelu_product(gate_hidden, up_hidden):
    return jax.nn.gelu(gate_hidden, approximate=False) * up_hidden


def contract_rows(left, right):
    return lax.dot_general(
        left, right, (((0,), (0,)), ((), ())), preferred_element_type=jnp.float32
    )


def contract_cols(left, right):
    return lax.dot_general(
        left, right, (((1,), (1,)), ((), ())), preferred_element_type=jnp.float32
    )


def rotate_pairs(values, angles):
    row_count, head_count, pair_width = values.shape
    paired = values.reshape(row_count, head_count, pair_width // 2, 2)
    first_part = paired[..., 0]
    second_part = paired[..., 1]
    cosine = jnp.cos(angles)[:, None, :]
    sine_part = jnp.sin(angles)[:, None, :]
    turned = jnp.stack(
        (
            first_part * cosine - second_part * sine_part,
            second_part * cosine + first_part * sine_part,
        ),
        axis=-1,
    )
    return turned.reshape(row_count, head_count, pair_width)


def retain(query_in, key_in, value_in, gate_in, first_head):
    row_count = query_in.shape[0]
    head_count = query_in.shape[1] // KEY_HEAD
    slot_count = row_count // SEQ
    block_len = min(512, SEQ // 2)
    block_count = SEQ // block_len
    position = (jnp.arange(row_count) % SEQ).astype(jnp.float32)
    angle_rate = 1.0 / 10000.0 ** jnp.linspace(0.0, 1.0, KEY_HEAD // 2)
    angles = position[:, None] * angle_rate[None, :]
    turned_query = rotate_pairs(query_in.reshape(row_count, head_count, KEY_HEAD), angles)
    turned_key = rotate_pairs(
        key_in.reshape(row_count, head_count, KEY_HEAD), angles
    ) * KEY_HEAD ** (-0.5)
    values_all = value_in.reshape(row_count, head_count, VAL_HEAD)
    head_ids = (first_head + jnp.arange(head_count)).astype(jnp.float32)
    log_decay = jnp.log(1.0 - 2.0 ** (-5.0 - head_ids))
    inner_index = jnp.arange(block_len).astype(jnp.float32)
    offset_grid = inner_index[:, None] - inner_index[None, :]
    within = jnp.where(
        offset_grid[None] >= 0,
        jnp.exp(jnp.maximum(offset_grid, 0.0)[None] * log_decay[:, None, None]),
        0.0,
    )
    query_scale = jnp.exp((inner_index[:, None] + 1.0) * log_decay[None, :])
    key_scale = jnp.exp((block_len - 1.0 - inner_index[:, None]) * log_decay[None, :])
    state_scale = jnp.exp(block_len * log_decay)

    def by_blocks(array_in):
        return array_in.reshape(
            slot_count, block_count, block_len, head_count, array_in.shape[-1]
        ).transpose(1, 0, 2, 3, 4)

    def advance(carry_state, block_parts):
        block_query, block_key, block_value = block_parts
        scores = (
            jnp.einsum("sihd,sjhd->shij", block_query, block_key, precision=three_pass)
            * within[None]
        )
        inside = jnp.einsum("shij,sjhe->sihe", scores, block_value, precision=three_pass)
        carried = jnp.einsum(
            "sihd,shde->sihe",
            block_query * query_scale[None, :, :, None],
            carry_state,
            precision=three_pass,
        )
        update = jnp.einsum(
            "sjhd,sjhe->shde",
            block_key * key_scale[None, :, :, None],
            block_value,
            precision=three_pass,
        )
        return (carry_state * state_scale[None, :, None, None] + update, inside + carried)

    start_state = jnp.zeros((slot_count, head_count, KEY_HEAD, VAL_HEAD), jnp.float32)
    _, mixed_heads = lax.scan(
        advance,
        start_state,
        (by_blocks(turned_query), by_blocks(turned_key), by_blocks(values_all)),
    )
    mixed_heads = mixed_heads.transpose(1, 0, 2, 3, 4).reshape(row_count, head_count, VAL_HEAD)
    centre = mixed_heads - jnp.mean(mixed_heads, axis=-1, keepdims=True)
    normed = centre * lax.rsqrt(jnp.maximum(jnp.mean(centre * centre, axis=-1, keepdims=True), 1.0))
    return jax.nn.silu(gate_in) * normed.reshape(row_count, head_count * VAL_HEAD)


def local(
    tokens,
    lengths,
    ln1_gain,
    ln1_bias,
    w_query,
    w_key,
    w_value,
    w_gate,
    w_out,
    ln2_gain,
    ln2_bias,
    mlp_gate,
    mlp_up,
    mlp_down,
    cotangent,
):
    own_rows = tokens.shape[0]
    tensor_rank = lax.axis_index("tensor")
    local_heads = w_query.shape[1] // KEY_HEAD
    first_head = tensor_rank * local_heads
    tokens_wide = tokens.astype(jnp.float32)
    normed_one, norm_one_back = jax.vjp(norm_rows, tokens_wide, ln1_gain, ln1_bias)
    sent_one = normed_one.astype(jnp.bfloat16)
    gathered_one = lax.all_gather(sent_one, "tensor", axis=0, tiled=True)
    query_low = jnp.dot(gathered_one, w_query, preferred_element_type=jnp.float32).astype(
        jnp.bfloat16
    )
    key_low = jnp.dot(gathered_one, w_key, preferred_element_type=jnp.float32).astype(jnp.bfloat16)
    value_low = jnp.dot(gathered_one, w_value, preferred_element_type=jnp.float32).astype(
        jnp.bfloat16
    )
    gate_low = jnp.dot(gathered_one, w_gate, preferred_element_type=jnp.float32).astype(
        jnp.bfloat16
    )

    def mix_heads(query_in, key_in, value_in, gate_in):
        return retain(query_in, key_in, value_in, gate_in, first_head)

    gated_out, mix_back = jax.vjp(
        mix_heads,
        query_low.astype(jnp.float32),
        key_low.astype(jnp.float32),
        value_low.astype(jnp.float32),
        gate_low.astype(jnp.float32),
    )
    gated_low = gated_out.astype(jnp.bfloat16)
    branch_one = lax.psum_scatter(
        jnp.dot(gated_low, w_out, preferred_element_type=jnp.float32).astype(jnp.bfloat16),
        "tensor",
        scatter_dimension=0,
        tiled=True,
    ).astype(jnp.float32)
    middle = tokens_wide + branch_one
    normed_two, norm_two_back = jax.vjp(norm_rows, middle, ln2_gain, ln2_bias)
    sent_two = normed_two.astype(jnp.bfloat16)
    gathered_two = lax.all_gather(sent_two, "tensor", axis=0, tiled=True)
    gate_hidden = jnp.dot(gathered_two, mlp_gate, preferred_element_type=jnp.float32)
    up_hidden = jnp.dot(gathered_two, mlp_up, preferred_element_type=jnp.float32)
    hidden, hidden_back = jax.vjp(gelu_product, gate_hidden, up_hidden)
    hidden_low = hidden.astype(jnp.bfloat16)
    branch_two = lax.psum_scatter(
        jnp.dot(hidden_low, mlp_down, preferred_element_type=jnp.float32).astype(jnp.bfloat16),
        "tensor",
        scatter_dimension=0,
        tiled=True,
    ).astype(jnp.float32)
    mixed_out = (middle + branch_two).astype(jnp.bfloat16)
    row_ids = tensor_rank * own_rows + jnp.arange(own_rows)
    slot_ids = row_ids // SEQ
    positions = row_ids % SEQ
    matches = slot_ids[:, None] == jnp.arange(lengths.shape[0])[None, :]
    limits = jnp.sum(jnp.where(matches, lengths[None, :], 0), axis=1)
    valid_rows = (positions < limits).astype(jnp.float32)
    out_grad = cotangent.astype(jnp.float32) * valid_rows[:, None]
    out_grad_low = out_grad.astype(jnp.bfloat16)
    gathered_grad_two = lax.all_gather(out_grad_low, "tensor", axis=0, tiled=True)
    grad_down = contract_rows(hidden_low, gathered_grad_two)
    grad_hidden = contract_cols(gathered_grad_two, mlp_down)
    grad_gate_wide, grad_up_wide = hidden_back(grad_hidden)
    grad_gate_hidden = grad_gate_wide.astype(jnp.bfloat16)
    grad_up_hidden = grad_up_wide.astype(jnp.bfloat16)
    grad_gate_weight = contract_rows(gathered_two, grad_gate_hidden)
    grad_up_weight = contract_rows(gathered_two, grad_up_hidden)
    grad_normed_two = lax.psum_scatter(
        (contract_cols(grad_gate_hidden, mlp_gate) + contract_cols(grad_up_hidden, mlp_up)).astype(
            jnp.bfloat16
        ),
        "tensor",
        scatter_dimension=0,
        tiled=True,
    ).astype(jnp.float32)
    grad_middle_norm, grad_gain_two, grad_bias_two = norm_two_back(grad_normed_two)
    grad_middle = out_grad + grad_middle_norm
    grad_branch = grad_middle.astype(jnp.bfloat16)
    gathered_grad_one = lax.all_gather(grad_branch, "tensor", axis=0, tiled=True)
    grad_out_weight = contract_rows(gated_low, gathered_grad_one)
    grad_gated = contract_cols(gathered_grad_one, w_out)
    grad_query_wide, grad_key_wide, grad_value_wide, grad_gate_proj_wide = mix_back(grad_gated)
    grad_query = grad_query_wide.astype(jnp.bfloat16)
    grad_key = grad_key_wide.astype(jnp.bfloat16)
    grad_value = grad_value_wide.astype(jnp.bfloat16)
    grad_gate = grad_gate_proj_wide.astype(jnp.bfloat16)
    grad_query_weight = contract_rows(gathered_one, grad_query)
    grad_key_weight = contract_rows(gathered_one, grad_key)
    grad_value_weight = contract_rows(gathered_one, grad_value)
    grad_gate_weight_one = contract_rows(gathered_one, grad_gate)
    total = contract_cols(grad_query, w_query)
    total = total + contract_cols(grad_key, w_key)
    total = total + contract_cols(grad_value, w_value)
    grad_normed_one = lax.psum_scatter(
        (total + contract_cols(grad_gate, w_gate)).astype(jnp.bfloat16),
        "tensor",
        scatter_dimension=0,
        tiled=True,
    ).astype(jnp.float32)
    grad_tokens_norm, grad_gain_one, grad_bias_one = norm_one_back(grad_normed_one)
    grad_tokens = grad_middle + grad_tokens_norm
    norm_terms = jnp.stack((grad_gain_one, grad_bias_one, grad_gain_two, grad_bias_two), axis=0)
    norm_summed = lax.psum_scatter(norm_terms, ("dp", "tensor"), scatter_dimension=1, tiled=True)
    summed_all = (
        lax.psum_scatter(
            grad_query_weight.astype(jnp.bfloat16), "dp", scatter_dimension=0, tiled=True
        ).astype(jnp.float32),
        lax.psum_scatter(
            grad_key_weight.astype(jnp.bfloat16), "dp", scatter_dimension=0, tiled=True
        ).astype(jnp.float32),
        lax.psum_scatter(
            grad_value_weight.astype(jnp.bfloat16), "dp", scatter_dimension=0, tiled=True
        ).astype(jnp.float32),
        lax.psum_scatter(
            grad_gate_weight_one.astype(jnp.bfloat16), "dp", scatter_dimension=0, tiled=True
        ).astype(jnp.float32),
        lax.psum_scatter(
            grad_out_weight.astype(jnp.bfloat16), "dp", scatter_dimension=1, tiled=True
        ).astype(jnp.float32),
        lax.psum_scatter(
            grad_gate_weight.astype(jnp.bfloat16), "dp", scatter_dimension=0, tiled=True
        ).astype(jnp.float32),
        lax.psum_scatter(
            grad_up_weight.astype(jnp.bfloat16), "dp", scatter_dimension=0, tiled=True
        ).astype(jnp.float32),
        lax.psum_scatter(
            grad_down.astype(jnp.bfloat16), "dp", scatter_dimension=1, tiled=True
        ).astype(jnp.float32),
    )
    return (
        mixed_out,
        grad_tokens,
        norm_summed[0],
        norm_summed[1],
        summed_all[0],
        summed_all[1],
        summed_all[2],
        summed_all[3],
        summed_all[4],
        norm_summed[2],
        norm_summed[3],
        summed_all[5],
        summed_all[6],
        summed_all[7],
    )


def solution(mesh):
    in_specs = (
        P(("dp", "tensor"), None),
        P("dp"),
        P(),
        P(),
        P(None, "tensor"),
        P(None, "tensor"),
        P(None, "tensor"),
        P(None, "tensor"),
        P("tensor", None),
        P(),
        P(),
        P(None, "tensor"),
        P(None, "tensor"),
        P("tensor", None),
        P(("dp", "tensor"), None),
    )
    out_specs = (
        P(("dp", "tensor"), None),
        P(("dp", "tensor"), None),
        P(("dp", "tensor")),
        P(("dp", "tensor")),
        P("dp", "tensor"),
        P("dp", "tensor"),
        P("dp", "tensor"),
        P("dp", "tensor"),
        P("tensor", "dp"),
        P(("dp", "tensor")),
        P(("dp", "tensor")),
        P("dp", "tensor"),
        P("dp", "tensor"),
        P("tensor", "dp"),
    )
    return jax.shard_map(local, mesh=mesh, in_specs=in_specs, out_specs=out_specs, check_vma=False)
```

profile of v0, /device:TPU:0, one launch (start us, length us, event | category | flops | bytes accessed | tf_op | source)
XLA Modules:
  0.0 1387.7 jit_solution(5816022111114414092)
XLA Ops:
  17.8 33.9 %all-gather.5.cloned.1.call-done = bf16[1024,2048]{1,0:T(8,128)(2,1)} async-done(((bf16[256,2048]{1,0:T(8,128)(2,1)}), bf16[1024,2048]{1,0:T(8,128)(2,1)}) %all-gather.5.cloned.1.call-update) | async-done | bytes 4194320 | tf_op jit(solution)/shard_map/all_gather | solution.py:141
  51.7 6.6 fusion.176
  61.7 5.9 fusion.175
  71.0 8.0 multiply_subtract_fusion
  82.2 4.7 reshape.836
  91.0 4.7 maximum_multiply_fusion
  95.7 4.8 mul.654
  104.7 9.9 convert_convert_fusion
  114.6 6.6 reshape.846
  121.2 5.1 copy.94
  129.3 32.9 %while.46 = (s32[]{:T(128)}, f32[1,2,256,512]{3,2,1,0:T(8,128)}, f32[2,1,512,2,512]{2,4,3,1,0:T(8,128)}, f32[2,1,2,512,512]{4,3,2,1,0:T(8,128)}, f32[2,1,512,2,2...) while((s32[]{:T(128)}, f32[1,2,256,512]{3,2,1,0:T(8,128)}, ...), condition=%wide.region_3.4_spmd.clone.clone.clone, body=%wide.region_2.3_spmd.clone.clone.clone.sunk | while | flops 4030990336 | bytes 124028416 | solution.py:106
  134.8 5.0 bitcast_dynamic-update-slice_fusion.9
  151.3 5.0 bitcast_dynamic-update-slice_fusion.9
  162.2 7.8 copy.96
  181.0 6.9 multiply_convert_fusion.2
  188.0 7.8 convolution_convert_fusion.7
  195.9 44.7 %reduce-scatter.16.cloned.1.call-done = bf16[256,2048]{1,0:T(8,128)(2,1)} async-done(((bf16[1024,2048]{1,0:T(8,128)(2,1)}), bf16[256,2048]{1,0:T(8,128)(2,1)}) %reduce-scatter.16.cloned.1.call-update) | async-done | bytes 1048592 | tf_op jit(solution)/shard_map/reduce_scatter | solution.py:164
  249.0 31.2 %all-gather.7.cloned.1.call-done = bf16[1024,2048]{1,0:T(8,128)(2,1)} async-done(((bf16[256,2048]{1,0:T(8,128)(2,1)}), bf16[1024,2048]{1,0:T(8,128)(2,1)}) %all-gather.7.cloned.1.call-update) | async-done | bytes 4194320 | tf_op jit(solution)/shard_map/all_gather | solution.py:173
  280.2 10.1 fusion.192
  290.3 26.4 %all-gather.9.cloned.1.call-done = bf16[1024,2048]{1,0:T(8,128)(2,1)} async-done(((bf16[256,2048]{1,0:T(8,128)(2,1)}), bf16[1024,2048]{1,0:T(8,128)(2,1)}) %all-gather.9.cloned.1.call-update) | async-done | bytes 4194320 | tf_op jit(solution)/shard_map/all_gather | solution.py:193
  316.7 19.2 %multiply_convert_fusion = (bf16[1024,1024]{0,1:T(8,128)(2,1)}, f32[1024,1024]{0,1:T(8,128)}, f32[1024,1024]{0,1:T(8,128)}) fusion(f32[1024,1024]{0,1:T(8,128)} %fusion.192, bf16[1024,2048]{1,0:T(8,128)(2,1)} %all-gather.9.cloned.1.call-done, bf16[1024,2048]{1,0:T(8,128)(2,1)} %param.32), kind=kOutput, calls=%fused_computation.146 | convolution fusion | flops 4364173312 | bytes 23068672 | tf_op jit(solution)/shard_map/dot_general | solution.py:30
  335.9 15.0 %add_convert_fusion.2 = (bf16[1024,1024]{0,1:T(8,128)(2,1)S(1)}, bf16[1024,1024]{0,1:T(8,128)(2,1)}) fusion(f32[1024,1024]{0,1:T(8,128)} %get-tuple-element.934, f32[1024,1024]{0,1:T(8,128)} %get-tuple-element.971, f32[1024,1024]{0,1:T(8,128)} %fusion.192, bf16[1024,2048]{1,0:T(8,128)(2,1)} %all-gather.7.cloned.1.call-done, bf16[2048,1024]{1,0:T(8,128)(2,1)} %param.31), kind=kOutput, calls=%fused_computation.147 | convolution fusion | flops 4313841664 | bytes 25165824 | tf_op jit(solution)/shard_map/dot_general | solution.py:175
  351.0 6.9 fusion.193
  357.9 8.4 add_convert_fusion.1
  366.5 9.7 convolution_convert_fusion.6
  376.3 34.7 %reduce-scatter.20.cloned.1.call-done = bf16[256,2048]{1,0:T(8,128)(2,1)} async-done(((bf16[1024,2048]{1,0:T(8,128)(2,1)}), bf16[256,2048]{1,0:T(8,128)(2,1)}) %reduce-scatter.20.cloned.1.call-update) | async-done | bytes 1048592 | tf_op jit(solution)/shard_map/reduce_scatter | solution.py:201
  414.1 43.9 %reduce-scatter.18.cloned.1.call-done = bf16[256,2048]{1,0:T(8,128)(2,1)} async-done(((bf16[1024,2048]{1,0:T(8,128)(2,1)}), bf16[256,2048]{1,0:T(8,128)(2,1)}) %reduce-scatter.18.cloned.1.call-update) | async-done | bytes 1048592 | tf_op jit(solution)/shard_map/reduce_scatter | solution.py:178
  464.6 9.6 convolution_convert_fusion.2
  474.5 9.5 convolution_convert_fusion.1
  484.1 5.3 copy.106
  489.4 9.3 convolution_convert_fusion
  499.3 14.0 %fusion.174 = (f32[1024,1024]{0,1:T(8,128)}, bf16[1024,1024]{0,1:T(8,128)(2,1)}) fusion(bf16[1024,1024]{0,1:T(8,128)(2,1)} %get-tuple-element.970, f32[1024,2]{0,1:T(2,128)S(1)} %rsqrt.35, f32[1024,1024]{0,1:T(8,128)} %bitcast.379, f32[1024,2]{0,1:T(2,128)S(1)} %bitcast.390, bf16[1024,2048]{1,0:T(8,128)(2,1)} %all-gather.11.cloned.1.call-done, ...), kind=kOutput, calls=%fused_computation.216 | convolution fusion | flops 4311744512 | bytes 20987904 | tf_op jit(solution)/shard_map/dot_general | solution.py:30
  513.2 6.6 reshape.837
  519.8 5.4 copy.107
  525.2 4.6 multiply_reduce_fusion
  543.1 107.8 %while.47 = (s32[]{:T(128)}, f32[1,2,256,512]{2,3,1,0:T(8,128)}, f32[2,1,512,2,256]{2,0,4,3,1:T(2,128)}, f32[2,1,512,2,256]{4,2,3,1,0:T(8,128)}, bf16[2,1,512,2,...) while((s32[]{:T(128)}, f32[1,2,256,512]{2,3,1,0:T(8,128)}, ...), condition=%wide.region_16.17_spmd.clone.clone.clone, body=%wide.region_15.16_spmd.clone.clone.clone.sunk | while | flops 8059095040 | bytes 142111728 | solution.py:106
  543.3 5.9 fusion.294
  558.7 19.7 %dynamic_update_slice.90 = f32[2,1,512,2,256]{2,0,4,3,1:T(2,128)} dynamic-update-slice(f32[2,1,512,2,256]{2,0,4,3,1:T(2,128)} %get-tuple-element.1279, f32[1,1,512,2,256]{2,0,4,3,1:T(1,128)} %copy.166, s32[]{:T(128)S(6)} %sub.300, s32[]{:T(128)} %constant.184.clone.1..sunk.1, s32[]{:T(128)} %constant.184.clone.1..sunk.1, s32[]{:T(128)} %constant.184.clone.1..sunk.1, s32[]{:T(128)} %constant.184.clone.1..sunk.1) | dynamic-update-slice | bytes 2097156 | tf_op jit(solution)/shard_map/transpose(jvp())/while/body/jit(dynamic_update_index_in_dim)/dynamic_update_slice | solution.py:106
  578.3 4.9 fusion.297
  595.5 5.9 fusion.294
  610.8 19.7 %dynamic_update_slice.90 = f32[2,1,512,2,256]{2,0,4,3,1:T(2,128)} dynamic-update-slice(f32[2,1,512,2,256]{2,0,4,3,1:T(2,128)} %get-tuple-element.1279, f32[1,1,512,2,256]{2,0,4,3,1:T(1,128)} %copy.166, s32[]{:T(128)S(6)} %sub.300, s32[]{:T(128)} %constant.184.clone.1..sunk.1, s32[]{:T(128)} %constant.184.clone.1..sunk.1, s32[]{:T(128)} %constant.184.clone.1..sunk.1, s32[]{:T(128)} %constant.184.clone.1..sunk.1) | dynamic-update-slice | bytes 2097156 | tf_op jit(solution)/shard_map/transpose(jvp())/while/body/jit(dynamic_update_index_in_dim)/dynamic_update_slice | solution.py:106
  630.5 4.9 fusion.297
  635.4 4.4 fusion.298
  654.0 4.2 copy.115
  658.2 4.8 mul.719
  663.0 4.8 transpose.140
  667.8 8.2 multiply_add_fusion.1
  678.9 6.4 convolution_convert_fusion.8
  690.8 6.6 convolution_convert_fusion.9
  704.9 7.0 fusion.195
  711.9 6.9 fusion.196
  718.8 12.0 add_convert_fusion
  730.9 9.3 convolution_convert_fusion.3
  740.5 9.4 convolution_convert_fusion.5
  750.0 9.5 convolution_convert_fusion.4
  764.2 10.5 reduce-scatter.38.cloned.1.call-done
  776.7 69.6 %reduce-scatter.26.cloned.1.call-done = bf16[256,512]{1,0:T(8,128)(2,1)} async-done(((bf16[2048,512]{1,0:T(8,128)(2,1)}), bf16[256,512]{1,0:T(8,128)(2,1)}) %reduce-scatter.26.cloned.1.call-update) | async-done | bytes 262160 | tf_op jit(solution)/shard_map/reduce_scatter | solution.py:241
  848.1 69.7 %reduce-scatter.24.cloned.1.call-done = bf16[256,512]{1,0:T(8,128)(2,1)} async-done(((bf16[2048,512]{1,0:T(8,128)(2,1)}), bf16[256,512]{1,0:T(8,128)(2,1)}) %reduce-scatter.24.cloned.1.call-update) | async-done | bytes 262160 | tf_op jit(solution)/shard_map/reduce_scatter | solution.py:238
  919.6 44.3 %reduce-scatter.22.cloned.1.call-done = bf16[256,2048]{1,0:T(8,128)(2,1)} async-done(((bf16[1024,2048]{1,0:T(8,128)(2,1)}), bf16[256,2048]{1,0:T(8,128)(2,1)}) %reduce-scatter.22.cloned.1.call-update) | async-done | bytes 1048592 | tf_op jit(solution)/shard_map/reduce_scatter | solution.py:227
  969.4 4.5 add_add_fusion.4
  974.0 82.1 %reduce-scatter.32.cloned.1.call-done = bf16[1024,256]{1,0:T(8,128)(2,1)} async-done(((bf16[1024,2048]{1,0:T(8,128)(2,1)}), bf16[1024,256]{1,0:T(8,128)(2,1)}) %reduce-scatter.32.cloned.1.call-update) | async-done | bytes 524304 | tf_op jit(solution)/shard_map/reduce_scatter | solution.py:250
  1058.2 89.3 %reduce-scatter.28.cloned.1.call-done = bf16[256,1024]{1,0:T(8,128)(2,1)} async-done(((bf16[2048,1024]{1,0:T(8,128)(2,1)}), bf16[256,1024]{1,0:T(8,128)(2,1)}) %reduce-scatter.28.cloned.1.call-update) | async-done | bytes 524304 | tf_op jit(solution)/shard_map/reduce_scatter | solution.py:244
  1149.6 89.4 %reduce-scatter.30.cloned.1.call-done = bf16[256,1024]{1,0:T(8,128)(2,1)} async-done(((bf16[2048,1024]{1,0:T(8,128)(2,1)}), bf16[256,1024]{1,0:T(8,128)(2,1)}) %reduce-scatter.30.cloned.1.call-update) | async-done | bytes 524304 | tf_op jit(solution)/shard_map/reduce_scatter | solution.py:247
  1241.2 136.1 %reduce-scatter.40.cloned.1.call-done = f32[64,4]{1,0:T(8,128)} async-done(((f32[2048,4]{1,0:T(8,128)}), f32[64,4]{1,0:T(8,128)}) %reduce-scatter.40.cloned.1.call-update) | async-done | bytes 1040
  (333 shorter events, 183.9 us)
Async XLA Ops:
  7.2 54.5 %copy-start = (bf16[2048,512]{1,0:T(8,128)(2,1)S(1)}, bf16[2048,512]{1,0:T(8,128)(2,1)}, u32[]{:S(2)}) copy-start(bf16[2048,512]{1,0:T(8,128)(2,1)} %param.23) | copy-start | bytes 6291460
  7.2 44.5 %all-gather.5.cloned.1.call-start = ((), (), s32[]{:S(2)}) async-start(), calls=%async_computation.13 | async-start | bytes 5242880 | tf_op jit(solution)/shard_map/all_gather | solution.py:141
  14.3 226.2 %reduce-scatter.16.cloned.1.call-start = ((), (), s32[]{:S(2)}) async-start(), calls=%async_computation.14 | async-start | bytes 5242880 | tf_op jit(solution)/shard_map/reduce_scatter | solution.py:164
  134.8 5.0 copy-start.10
  134.8 5.0 copy-start.30
  151.3 5.0 copy-start.10
  151.3 5.0 copy-start.30
  162.2 7.9 copy-start.5
  162.2 7.8 copy-start.15
  162.2 7.8 copy-start.47
  162.2 7.8 copy-start.49
  162.2 7.8 copy-start.51
  176.0 5.0 copy-start.40
  177.1 10.9 copy-start.17
  181.0 6.9 copy-start.42
  195.8 44.8 %copy-start.12 = (bf16[256,2048]{1,0:T(8,128)(2,1)S(1)}, bf16[256,2048]{1,0:T(8,128)(2,1)}, u32[]{:S(2)}) copy-start(bf16[256,2048]{1,0:T(8,128)(2,1)} %param.19) | copy-start | bytes 3145732
  195.8 48.2 %copy-start.54 = (f32[2048]{0:T(1024)S(1)}, f32[2048]{0:T(1024)}, u32[]{:S(2)}) copy-start(f32[2048]{0:T(1024)} %param.28) | copy-start | bytes 24580
  195.8 48.2 %copy-start.67 = (f32[2048]{0:T(1024)S(1)}, f32[2048]{0:T(1024)}, u32[]{:S(2)}) copy-start(f32[2048]{0:T(1024)} %param.29) | copy-start | bytes 24580
  195.8 84.4 %all-gather.7.cloned.1.call-start = ((), (), s32[]{:S(2)}) async-start(), calls=%async_computation.15 | async-start | bytes 5242880 | tf_op jit(solution)/shard_map/all_gather | solution.py:173
  245.6 71.1 %all-gather.9.cloned.1.call-start = ((), (), s32[]{:S(2)}) async-start(), calls=%async_computation.17 | async-start | bytes 5242880 | tf_op jit(solution)/shard_map/all_gather | solution.py:193
  246.5 215.3 %copy-start.61 = (f32[256]{0:T(256)}, f32[256]{0:T(256)S(1)}, u32[]{:S(2)}) copy-start(f32[256]{0:T(256)S(1)} %compare_convert_fusion) | copy-start | bytes 3076
  249.0 162.0 %reduce-scatter.20.cloned.1.call-start = ((), (), s32[]{:S(2)}) async-start(), calls=%async_computation.18 | async-start | bytes 5242880 | tf_op jit(solution)/shard_map/reduce_scatter | solution.py:201
  335.9 15.1 %copy-start.68 = (bf16[2048,1024]{1,0:T(8,128)(2,1)S(1)}, bf16[2048,1024]{1,0:T(8,128)(2,1)}, u32[]{:S(2)}) copy-start(bf16[2048,1024]{1,0:T(8,128)(2,1)} %param.30) | copy-start | bytes 12582916
  350.9 6.9 copy-start.71
  350.9 6.9 copy-start.69
  350.9 6.9 copy-start.72
  366.3 91.7 %reduce-scatter.18.cloned.1.call-start = ((), (), s32[]{:S(2)}) async-start(), calls=%async_computation.16 | async-start | bytes 5242880 | tf_op jit(solution)/shard_map/reduce_scatter | solution.py:178
  376.2 123.0 %all-gather.11.cloned.1.call-start = ((), (), s32[]{:S(2)}) async-start(), calls=%async_computation.19 | async-start | bytes 5242880 | tf_op jit(solution)/shard_map/all_gather | solution.py:212
  458.0 5.2 copy-start.33
  461.8 12.4 copy-start.65
  464.6 295.3 %reduce-scatter.34.cloned.1.call-start = ((), (), s32[]{:S(2)}) async-start(), calls=%async_computation.26 | async-start | bytes 4718592 | tf_op jit(solution)/shard_map/reduce_scatter | solution.py:253
  474.3 287.8 %reduce-scatter.36.cloned.1.call-start = ((), (), s32[]{:S(2)}) async-start(), calls=%async_computation.27 | async-start | bytes 4718592 | tf_op jit(solution)/shard_map/reduce_scatter | solution.py:256
  484.1 290.6 %reduce-scatter.38.cloned.1.call-start = ((), (), s32[]{:S(2)}) async-start(), calls=%async_computation.28 | async-start | bytes 4718592 | tf_op jit(solution)/shard_map/reduce_scatter | solution.py:259
  498.8 347.5 %reduce-scatter.26.cloned.1.call-start = ((), (), s32[]{:S(2)}) async-start(), calls=%async_computation.22 | async-start | bytes 2359296 | tf_op jit(solution)/shard_map/reduce_scatter | solution.py:241
  525.2 6.3 copy-start.19
  538.1 5.0 copy-start.16
  538.1 5.0 copy-start.48
  538.1 5.0 copy-start.50
  538.1 5.0 copy-start.52
  543.3 7.3 copy-start.9
  543.3 8.7 copy-start.32
  595.5 7.2 copy-start.9
  595.5 8.6 copy-start.32
  658.2 9.6 copy-start.36
  658.2 9.6 copy-start.37
  678.9 6.5 copy-start.41
  685.3 232.5 %reduce-scatter.24.cloned.1.call-start = ((), (), s32[]{:S(2)}) async-start(), calls=%async_computation.21 | async-start | bytes 2359296 | tf_op jit(solution)/shard_map/reduce_scatter | solution.py:238
  690.8 6.6 copy-start.45
  697.4 266.5 %reduce-scatter.22.cloned.1.call-start = ((), (), s32[]{:S(2)}) async-start(), calls=%async_computation.20 | async-start | bytes 5242880 | tf_op jit(solution)/shard_map/reduce_scatter | solution.py:227
  704.9 7.0 copy-start.39
  704.9 7.0 copy-start.43
  730.8 325.3 %reduce-scatter.32.cloned.1.call-start = ((), (), s32[]{:S(2)}) async-start(), calls=%async_computation.25 | async-start | bytes 4718592 | tf_op jit(solution)/shard_map/reduce_scatter | solution.py:250
  740.2 407.3 %reduce-scatter.28.cloned.1.call-start = ((), (), s32[]{:S(2)}) async-start(), calls=%async_computation.23 | async-start | bytes 4718592 | tf_op jit(solution)/shard_map/reduce_scatter | solution.py:244
  749.9 489.1 %reduce-scatter.30.cloned.1.call-start = ((), (), s32[]{:S(2)}) async-start(), calls=%async_computation.24 | async-start | bytes 4718592 | tf_op jit(solution)/shard_map/reduce_scatter | solution.py:247
  759.5 204.4 %copy-start.13 = (bf16[256,2048]{1,0:T(8,128)(2,1)S(1)}, bf16[256,2048]{1,0:T(8,128)(2,1)}, u32[]{:S(2)}) copy-start(bf16[256,2048]{1,0:T(8,128)(2,1)} %param.19) | copy-start | bytes 3145732
  759.5 204.3 %copy-start.53 = (f32[2048]{0:T(1024)S(1)}, f32[2048]{0:T(1024)}, u32[]{:S(2)}) copy-start(f32[2048]{0:T(1024)} %param.21) | copy-start | bytes 24580
  759.5 204.3 %copy-start.56 = (f32[256]{0:T(256)S(1)}, f32[256]{0:T(256)}, u32[]{:S(2)}) copy-start(f32[256]{0:T(256)} %copy-done.55) | copy-start | bytes 3076
  759.6 206.1 %copy-start.64 = (f32[256]{0:T(256)S(1)}, f32[256]{0:T(256)}, u32[]{:S(2)}) copy-start(f32[256]{0:T(256)} %copy-done.63) | copy-start | bytes 3076
  759.6 206.1 %copy-start.60 = (f32[256]{0:T(256)S(1)}, f32[256]{0:T(256)}, u32[]{:S(2)}) copy-start(f32[256]{0:T(256)} %copy-done.59) | copy-start | bytes 3076
  759.6 617.8 %reduce-scatter.40.cloned.1.call-start = ((), (), s32[]{:S(2)}) async-start(), calls=%async_computation.29 | async-start | bytes 1081344
  762.0 206.0 %copy-start.57 = (f32[2048]{0:T(1024)S(1)}, f32[2048]{0:T(1024)}, u32[]{:S(2)}) copy-start(f32[2048]{0:T(1024)} %get-tuple-element.855) | copy-start | bytes 24580
  762.0 206.0 %copy-start.58 = (f32[2048]{0:T(1024)S(1)}, f32[2048]{0:T(1024)}, u32[]{:S(2)}) copy-start(f32[2048]{0:T(1024)} %get-tuple-element.860) | copy-start | bytes 24580
  776.7 192.7 %copy-start.62 = (f32[256]{0:T(256)S(1)}, f32[256]{0:T(256)}, u32[]{:S(2)}) copy-start(f32[256]{0:T(256)} %copy-done.61) | copy-start | bytes 3076
  776.7 192.7 %copy-start.66 = (f32[256]{0:T(256)S(1)}, f32[256]{0:T(256)}, u32[]{:S(2)}) copy-start(f32[256]{0:T(256)} %copy-done.65) | copy-start | bytes 3076
  (46 other events, 127.1 us)
Sparse Core Ops, SparseCore 0:
  14.5 37.1 all-gather.4
  196.0 44.5 reduce-scatter.15
  245.7 34.4 all-gather.6
  282.2 34.4 all-gather.8
  366.4 44.5 reduce-scatter.19
  413.4 44.5 reduce-scatter.17
  464.7 34.4 all-gather.10
  502.8 88.2 reduce-scatter.33
  594.8 87.9 reduce-scatter.35
  686.3 88.3 reduce-scatter.37
  778.2 68.0 reduce-scatter.25
  850.3 67.4 reduce-scatter.23
  920.3 43.5 reduce-scatter.21
  967.4 88.6 reduce-scatter.31
  1059.6 87.8 reduce-scatter.27
  1151.0 88.0 reduce-scatter.29
  1241.2 136.1 reduce-scatter.39
where the time goes:
time: 1400 us; the launch traced here: 1390 us
  waiting for transfers between devices  806 us (58%)
  matrix products  297 us (21%)
  local copies, waits for them, and re-layouts  167 us (12%)
  other arithmetic  98.3 us (7%)
  between operations  15.7 us (1%)
    unnamed x18, waiting for transfers between devices  136 us
    reduce_scatter x1, waiting for transfers between devices, local(): lax.psum_scatter(grad_gate_weight_one.astype(jnp.bfloat16), 'dp', scatter...  89.4 us
    reduce_scatter x1, waiting for transfers between devices, local(): lax.psum_scatter(grad_value_weight.astype(jnp.bfloat16), 'dp', scatter_di...  89.3 us
    reduce_scatter x1, waiting for transfers between devices, local(): lax.psum_scatter(grad_out_weight.astype(jnp.bfloat16), 'dp', scatter_dime...  82.1 us
    dot_general x8, matrix products, contract_cols(): lax.dot_general(left, right, (((1,), (1,)), ((), ())), preferred_element_...  76.7 us
    reduce_scatter x1, waiting for transfers between devices, local(): lax.psum_scatter(grad_query_weight.astype(jnp.bfloat16), 'dp', scatter_di...  69.7 us
    dot_general x8, matrix products, contract_rows(): lax.dot_general(left, right, (((0,), (0,)), ((), ())), preferred_element_...  69.7 us
    reduce_scatter x1, waiting for transfers between devices, local(): lax.psum_scatter(grad_key_weight.astype(jnp.bfloat16), 'dp', scatter_dime...  69.6 us
  transfers between devices with their start and end apart: 17, of which 14 were waited for; matrix products, arithmetic and copies ran while one was open for 24% of the time, Pallas kernels for 0%

commit v1 on v0

--- a/solution.py
+++ b/solution.py
@@ -8,6 +8,18 @@
 SEQ = 1024
 epsilon = 1e-05
 three_pass = lax.Precision.HIGH
+
+
+def doubled_up(x, axis, dim):
+    ways, here = (lax.axis_size(axis), lax.axis_index(axis))
+    grown, reach = (x, 1)
+    while reach < ways:
+        theirs = lax.ppermute(grown, axis, [(d, d ^ reach) for d in range(ways)])
+        mine_first = jnp.concatenate([grown, theirs], axis=dim)
+        theirs_first = jnp.concatenate([theirs, grown], axis=dim)
+        grown = jnp.where(here & reach == 0, mine_first, theirs_first)
+        reach = 2 * reach
+    return grown
 
 
 def norm_rows(values, gain_in, bias_in):
@@ -170,7 +182,7 @@
     middle = tokens_wide + branch_one
     normed_two, norm_two_back = jax.vjp(norm_rows, middle, ln2_gain, ln2_bias)
     sent_two = normed_two.astype(jnp.bfloat16)
-    gathered_two = lax.all_gather(sent_two, "tensor", axis=0, tiled=True)
+    gathered_two = doubled_up(sent_two, "tensor", 0)
     gate_hidden = jnp.dot(gathered_two, mlp_gate, preferred_element_type=jnp.float32)
     up_hidden = jnp.dot(gathered_two, mlp_up, preferred_element_type=jnp.float32)
     hidden, hidden_back = jax.vjp(gelu_product, gate_hidden, up_hidden)

time: 1400 us -> 1420 us (1.014)
    ppermute x0 -> x2, waiting for transfers between devices: none -> 69.9 us  [doubled_up(): theirs = lax.ppermute(grown, axis, [(d, d ^ reach) for d in range(ways)])]
    all_gather x1 -> x0, waiting for transfers between devices: 31.2 us -> none  [local(): gathered_two = lax.all_gather(sent_two, 'tensor', axis=0, tiled=True)]
    all_gather x1, waiting for transfers between devices: 26.4 us -> 0.01 us  [local(): lax.all_gather(out_grad_low, 'tensor', axis=0, tiled=True)]
    unnamed x18 -> x17, waiting for transfers between devices: 136 us -> 136 us
    unnamed x116 -> x120, local copies, waits for them, and re-layouts: 30.1 us -> 30.1 us
  transfers between devices with their start and end apart: 17 -> 18, of which waited for: 14 -> 14; matrix products, arithmetic and copies ran while one was open for 24% -> 25% of each run, Pallas kernels for 0% -> 0%
where the time goes in v1:
time: 1420 us; the launch traced here: 1400 us
  waiting for transfers between devices  813 us (57%)
  matrix products  298 us (21%)
  local copies, waits for them, and re-layouts  167 us (12%)
  other arithmetic  103 us (7%)
  between operations  15.8 us (1%)
    unnamed x17, waiting for transfers between devices  136 us
    reduce_scatter x1, waiting for transfers between devices, local(): lax.psum_scatter(grad_gate_weight_one.astype(jnp.bfloat16), 'dp', scatter...  89.4 us
    reduce_scatter x1, waiting for transfers between devices, local(): lax.psum_scatter(grad_value_weight.astype(jnp.bfloat16), 'dp', scatter_di...  89.4 us
    reduce_scatter x1, waiting for transfers between devices, local(): lax.psum_scatter(grad_out_weight.astype(jnp.bfloat16), 'dp', scatter_dime...  82.3 us
    dot_general x8, matrix products, contract_cols(): lax.dot_general(left, right, (((1,), (1,)), ((), ())), preferred_element_...  74.9 us
    dot_general x8, matrix products, contract_rows(): lax.dot_general(left, right, (((0,), (0,)), ((), ())), preferred_element_...  72.2 us
    ppermute x2, waiting for transfers between devices, doubled_up(): theirs = lax.ppermute(grown, axis, [(d, d ^ reach) for d in range(ways)])  69.9 us
    reduce_scatter x1, waiting for transfers between devices, local(): lax.psum_scatter(grad_query_weight.astype(jnp.bfloat16), 'dp', scatter_di...  69.9 us
  transfers between devices with their start and end apart: 18, of which 14 were waited for; matrix products, arithmetic and copies ran while one was open for 25% of the time, Pallas kernels for 0%

profile of v1, /device:TPU:0, one launch (start us, length us, event | category | flops | bytes accessed | tf_op | source)
XLA Modules:
  0.0 1400.8 jit_solution(15158475671199421565)
XLA Ops:
  17.8 33.9 %all-gather.4.cloned.1.call-done = bf16[1024,2048]{1,0:T(8,128)(2,1)} async-done(((bf16[256,2048]{1,0:T(8,128)(2,1)}), bf16[1024,2048]{1,0:T(8,128)(2,1)}) %all-gather.4.cloned.1.call-update) | async-done | bytes 4194320 | tf_op jit(solution)/shard_map/all_gather | solution.py:153
  51.7 6.6 fusion.176
  61.7 5.9 fusion.175
  71.0 7.9 multiply_subtract_fusion
  82.2 4.7 reshape.836
  91.0 4.5 maximum_multiply_fusion
  95.5 4.8 mul.654
  104.5 9.9 convert_convert_fusion
  114.4 6.6 reshape.846
  121.1 5.0 copy.94
  129.1 33.2 %while.46 = (s32[]{:T(128)}, f32[1,2,256,512]{3,2,1,0:T(8,128)}, f32[2,1,512,2,512]{2,4,3,1,0:T(8,128)}, f32[2,1,2,512,512]{4,3,2,1,0:T(8,128)}, f32[2,1,512,2,2...) while((s32[]{:T(128)}, f32[1,2,256,512]{3,2,1,0:T(8,128)}, ...), condition=%wide.region_3.4_spmd.clone.clone.clone, body=%wide.region_2.3_spmd.clone.clone.clone.sunk | while | flops 4030990336 | bytes 124028416 | solution.py:118
  134.9 4.9 bitcast_dynamic-update-slice_fusion.9
  151.4 4.9 bitcast_dynamic-update-slice_fusion.9
  162.3 7.9 copy.96
  181.2 6.9 multiply_convert_fusion.2
  188.2 7.9 convolution_convert_fusion.7
  199.6 41.2 %reduce-scatter.16.cloned.1.call-done = bf16[256,2048]{1,0:T(8,128)(2,1)} async-done(((bf16[1024,2048]{1,0:T(8,128)(2,1)}), bf16[256,2048]{1,0:T(8,128)(2,1)}) %reduce-scatter.16.cloned.1.call-update) | async-done | bytes 1048592 | tf_op jit(solution)/shard_map/reduce_scatter | solution.py:176
  248.8 5.0 maximum_select_fusion.1
  253.9 66.9 %collective-permute-done.1 = bf16[512,2048]{1,0:T(8,128)(2,1)} collective-permute-done((bf16[512,2048]{1,0:T(8,128)(2,1)}, bf16[512,2048]{1,0:T(8,128)(2,1)}, u32[]{:S(2)}, u32[]{:S(2)}) %collective-permute-start.1) | collective-permute-done | bytes 2097184 | tf_op jit(solution)/shard_map/ppermute | solution.py:17
  320.9 11.3 fusion.190
  332.2 19.3 %multiply_convert_fusion = (bf16[1024,1024]{0,1:T(8,128)(2,1)}, f32[1024,1024]{0,1:T(8,128)}, f32[1024,1024]{0,1:T(8,128)}) fusion(f32[1024,1024]{0,1:T(8,128)} %fusion.190, bf16[1024,2048]{1,0:T(8,128)(2,1)} %all-gather.6.cloned.1.call-done, bf16[1024,2048]{1,0:T(8,128)(2,1)} %param.32), kind=kOutput, calls=%fused_computation.147 | convolution fusion | flops 4364173312 | bytes 23068672 | tf_op jit(solution)/shard_map/dot_general | solution.py:42
  351.4 14.1 %add_convert_fusion.2 = (bf16[1024,1024]{0,1:T(8,128)(2,1)}, bf16[1024,1024]{0,1:T(8,128)(2,1)}) fusion(f32[1024,1024]{0,1:T(8,128)} %get-tuple-element.934, f32[1024,1024]{0,1:T(8,128)} %get-tuple-element.971, f32[1024,1024]{0,1:T(8,128)} %fusion.190, bf16[2048,1024]{1,0:T(8,128)(2,1)} %param.31, bf16[512,2048]{1,0:T(8,128)(2,1)} %collective-permute-done.1, ...), kind=kOutput, calls=%fused_computation.148 | convolution fusion | flops 4332716032 | bytes 25165824 | tf_op jit(solution)/shard_map/dot_general | solution.py:187
  365.6 7.3 fusion.194
  373.0 6.3 add_convert_fusion.1
  379.3 9.8 convolution_convert_fusion.6
  389.2 34.8 %reduce-scatter.20.cloned.1.call-done = bf16[256,2048]{1,0:T(8,128)(2,1)} async-done(((bf16[1024,2048]{1,0:T(8,128)(2,1)}), bf16[256,2048]{1,0:T(8,128)(2,1)}) %reduce-scatter.20.cloned.1.call-update) | async-done | bytes 1048592 | tf_op jit(solution)/shard_map/reduce_scatter | solution.py:213
  427.1 43.9 %reduce-scatter.18.cloned.1.call-done = bf16[256,2048]{1,0:T(8,128)(2,1)} async-done(((bf16[1024,2048]{1,0:T(8,128)(2,1)}), bf16[256,2048]{1,0:T(8,128)(2,1)}) %reduce-scatter.18.cloned.1.call-update) | async-done | bytes 1048592 | tf_op jit(solution)/shard_map/reduce_scatter | solution.py:190
  477.8 10.8 convolution_convert_fusion.1
  488.7 10.9 convolution_convert_fusion.2
  499.6 5.3 copy.106
  504.9 9.3 convolution_convert_fusion
  514.8 14.0 fusion.174
  528.8 6.7 reshape.837
  535.4 5.4 copy.107
  540.8 4.6 multiply_reduce_fusion
  558.8 107.9 %while.47 = (s32[]{:T(128)}, f32[1,2,256,512]{2,3,1,0:T(8,128)}, f32[2,1,512,2,256]{2,0,4,3,1:T(2,128)}, f32[2,1,512,2,256]{4,2,3,1,0:T(8,128)}, bf16[2,1,512,2,...) while((s32[]{:T(128)}, f32[1,2,256,512]{2,3,1,0:T(8,128)}, ...), condition=%wide.region_16.17_spmd.clone.clone.clone, body=%wide.region_15.16_spmd.clone.clone.clone.sunk | while | flops 8059095040 | bytes 142111728 | solution.py:118
  559.0 6.0 fusion.291
  574.4 19.6 %dynamic_update_slice.90 = f32[2,1,512,2,256]{2,0,4,3,1:T(2,128)} dynamic-update-slice(f32[2,1,512,2,256]{2,0,4,3,1:T(2,128)} %get-tuple-element.1279, f32[1,1,512,2,256]{2,0,4,3,1:T(1,128)} %copy.166, s32[]{:T(128)S(6)} %sub.300, s32[]{:T(128)} %constant.185.clone.1..sunk.1, s32[]{:T(128)} %constant.185.clone.1..sunk.1, s32[]{:T(128)} %constant.185.clone.1..sunk.1, s32[]{:T(128)} %constant.185.clone.1..sunk.1) | dynamic-update-slice | bytes 2097156 | tf_op jit(solution)/shard_map/transpose(jvp())/while/body/jit(dynamic_update_index_in_dim)/dynamic_update_slice | solution.py:118
  594.1 4.9 fusion.294
  611.3 5.9 fusion.291
  626.6 19.6 %dynamic_update_slice.90 = f32[2,1,512,2,256]{2,0,4,3,1:T(2,128)} dynamic-update-slice(f32[2,1,512,2,256]{2,0,4,3,1:T(2,128)} %get-tuple-element.1279, f32[1,1,512,2,256]{2,0,4,3,1:T(1,128)} %copy.166, s32[]{:T(128)S(6)} %sub.300, s32[]{:T(128)} %constant.185.clone.1..sunk.1, s32[]{:T(128)} %constant.185.clone.1..sunk.1, s32[]{:T(128)} %constant.185.clone.1..sunk.1, s32[]{:T(128)} %constant.185.clone.1..sunk.1) | dynamic-update-slice | bytes 2097156 | tf_op jit(solution)/shard_map/transpose(jvp())/while/body/jit(dynamic_update_index_in_dim)/dynamic_update_slice | solution.py:118
  646.3 4.9 fusion.294
  651.2 4.4 fusion.295
  669.7 4.1 copy.115
  673.9 4.8 mul.719
  678.7 4.8 transpose.140
  683.5 8.1 multiply_add_fusion.1
  694.5 6.4 convolution_convert_fusion.8
  706.4 6.3 convolution_convert_fusion.9
  720.3 6.9 fusion.196
  727.1 6.8 fusion.197
  733.9 12.0 add_convert_fusion
  746.0 9.3 convolution_convert_fusion.3
  755.6 9.4 convolution_convert_fusion.5
  765.1 9.9 convolution_convert_fusion.4
  779.7 8.1 reduce-scatter.38.cloned.1.call-done
  789.9 69.2 %reduce-scatter.26.cloned.1.call-done = bf16[256,512]{1,0:T(8,128)(2,1)} async-done(((bf16[2048,512]{1,0:T(8,128)(2,1)}), bf16[256,512]{1,0:T(8,128)(2,1)}) %reduce-scatter.26.cloned.1.call-update) | async-done | bytes 262160 | tf_op jit(solution)/shard_map/reduce_scatter | solution.py:253
  860.9 69.9 %reduce-scatter.24.cloned.1.call-done = bf16[256,512]{1,0:T(8,128)(2,1)} async-done(((bf16[2048,512]{1,0:T(8,128)(2,1)}), bf16[256,512]{1,0:T(8,128)(2,1)}) %reduce-scatter.24.cloned.1.call-update) | async-done | bytes 262160 | tf_op jit(solution)/shard_map/reduce_scatter | solution.py:250
  932.7 44.3 %reduce-scatter.22.cloned.1.call-done = bf16[256,2048]{1,0:T(8,128)(2,1)} async-done(((bf16[1024,2048]{1,0:T(8,128)(2,1)}), bf16[256,2048]{1,0:T(8,128)(2,1)}) %reduce-scatter.22.cloned.1.call-update) | async-done | bytes 1048592 | tf_op jit(solution)/shard_map/reduce_scatter | solution.py:239
  982.5 4.5 add_add_fusion.4
  987.0 82.3 %reduce-scatter.32.cloned.1.call-done = bf16[1024,256]{1,0:T(8,128)(2,1)} async-done(((bf16[1024,2048]{1,0:T(8,128)(2,1)}), bf16[1024,256]{1,0:T(8,128)(2,1)}) %reduce-scatter.32.cloned.1.call-update) | async-done | bytes 524304 | tf_op jit(solution)/shard_map/reduce_scatter | solution.py:262
  1071.4 89.4 %reduce-scatter.28.cloned.1.call-done = bf16[256,1024]{1,0:T(8,128)(2,1)} async-done(((bf16[2048,1024]{1,0:T(8,128)(2,1)}), bf16[256,1024]{1,0:T(8,128)(2,1)}) %reduce-scatter.28.cloned.1.call-update) | async-done | bytes 524304 | tf_op jit(solution)/shard_map/reduce_scatter | solution.py:256
  1162.9 89.4 %reduce-scatter.30.cloned.1.call-done = bf16[256,1024]{1,0:T(8,128)(2,1)} async-done(((bf16[2048,1024]{1,0:T(8,128)(2,1)}), bf16[256,1024]{1,0:T(8,128)(2,1)}) %reduce-scatter.30.cloned.1.call-update) | async-done | bytes 524304 | tf_op jit(solution)/shard_map/reduce_scatter | solution.py:259
  1254.4 136.1 %reduce-scatter.40.cloned.1.call-done = f32[64,4]{1,0:T(8,128)} async-done(((f32[2048,4]{1,0:T(8,128)}), f32[64,4]{1,0:T(8,128)}) %reduce-scatter.40.cloned.1.call-update) | async-done | bytes 1040
  (339 shorter events, 187.1 us)
Async XLA Ops:
  7.2 54.5 %copy-start = (bf16[2048,512]{1,0:T(8,128)(2,1)S(1)}, bf16[2048,512]{1,0:T(8,128)(2,1)}, u32[]{:S(2)}) copy-start(bf16[2048,512]{1,0:T(8,128)(2,1)} %param.23) | copy-start | bytes 6291460
  7.2 44.5 %all-gather.4.cloned.1.call-start = ((), (), s32[]{:S(2)}) async-start(), calls=%async_computation.13 | async-start | bytes 5242880 | tf_op jit(solution)/shard_map/all_gather | solution.py:153
  14.4 226.4 %reduce-scatter.16.cloned.1.call-start = ((), (), s32[]{:S(2)}) async-start(), calls=%async_computation.14 | async-start | bytes 5242880 | tf_op jit(solution)/shard_map/reduce_scatter | solution.py:176
  134.9 4.9 copy-start.10
  134.9 4.9 copy-start.30
  151.4 4.9 copy-start.30
  162.2 7.9 copy-start.5
  162.2 7.9 copy-start.15
  162.2 7.9 copy-start.47
  162.3 7.9 copy-start.49
  162.3 7.9 copy-start.51
  176.3 5.0 copy-start.40
  177.3 10.9 copy-start.17
  181.2 6.9 copy-start.42
  196.0 44.8 %copy-start.12 = (bf16[256,2048]{1,0:T(8,128)(2,1)S(1)}, bf16[256,2048]{1,0:T(8,128)(2,1)}, u32[]{:S(2)}) copy-start(bf16[256,2048]{1,0:T(8,128)(2,1)} %param.19) | copy-start | bytes 3145732
  196.1 48.1 %copy-start.58 = (f32[2048]{0:T(1024)S(1)}, f32[2048]{0:T(1024)}, u32[]{:S(2)}) copy-start(f32[2048]{0:T(1024)} %param.28) | copy-start | bytes 24580
  196.1 48.1 %copy-start.71 = (f32[2048]{0:T(1024)S(1)}, f32[2048]{0:T(1024)}, u32[]{:S(2)}) copy-start(f32[2048]{0:T(1024)} %param.29) | copy-start | bytes 24580
  196.1 136.1 %all-gather.6.cloned.1.call-start = ((), (), s32[]{:S(2)}) async-start(), calls=%async_computation.16 | async-start | bytes 5242880 | tf_op jit(solution)/shard_map/all_gather | solution.py:205
  196.9 278.0 %copy-start.65 = (f32[256]{0:T(256)}, f32[256]{0:T(256)S(1)}, u32[]{:S(2)}) copy-start(f32[256]{0:T(256)S(1)} %compare_convert_fusion) | copy-start | bytes 3076
  199.4 224.6 %reduce-scatter.20.cloned.1.call-start = ((), (), s32[]{:S(2)}) async-start(), calls=%async_computation.17 | async-start | bytes 5242880 | tf_op jit(solution)/shard_map/reduce_scatter | solution.py:213
  245.8 3.0 collective-permute-start
  253.8 67.1 %collective-permute-start.1 = (bf16[512,2048]{1,0:T(8,128)(2,1)}, bf16[512,2048]{1,0:T(8,128)(2,1)}, u32[]{:S(2)}, u32[]{:S(2)}) collective-permute-start(bf16[512,2048]{1,0:T(8,128)(2,1)} %maximum_select_fusion.1), channel_id=1, source_target_pairs={{0,2},{1,3},{2,0},{3,1},{4,6},{5,7},{6,4},{7,5},{8,10},{9,11},{10,... | collective-permute-start | bytes 6291464 | tf_op jit(solution)/shard_map/ppermute | solution.py:17
  365.6 7.4 copy-start.72
  365.6 7.4 copy-start.74
  379.3 91.7 %reduce-scatter.18.cloned.1.call-start = ((), (), s32[]{:S(2)}) async-start(), calls=%async_computation.15 | async-start | bytes 5242880 | tf_op jit(solution)/shard_map/reduce_scatter | solution.py:190
  389.1 125.7 %all-gather.8.cloned.1.call-start = ((), (), s32[]{:S(2)}) async-start(), calls=%async_computation.18 | async-start | bytes 5242880 | tf_op jit(solution)/shard_map/all_gather | solution.py:224
  471.0 5.2 copy-start.33
  474.8 13.8 copy-start.69
  477.6 297.8 %reduce-scatter.36.cloned.1.call-start = ((), (), s32[]{:S(2)}) async-start(), calls=%async_computation.26 | async-start | bytes 4718592 | tf_op jit(solution)/shard_map/reduce_scatter | solution.py:268
  488.6 288.9 %reduce-scatter.34.cloned.1.call-start = ((), (), s32[]{:S(2)}) async-start(), calls=%async_computation.25 | async-start | bytes 4718592 | tf_op jit(solution)/shard_map/reduce_scatter | solution.py:265
  499.6 288.2 %reduce-scatter.38.cloned.1.call-start = ((), (), s32[]{:S(2)}) async-start(), calls=%async_computation.27 | async-start | bytes 4718592 | tf_op jit(solution)/shard_map/reduce_scatter | solution.py:271
  514.2 344.9 %reduce-scatter.26.cloned.1.call-start = ((), (), s32[]{:S(2)}) async-start(), calls=%async_computation.21 | async-start | bytes 2359296 | tf_op jit(solution)/shard_map/reduce_scatter | solution.py:253
  540.8 5.0 copy-start.18
  540.8 6.3 copy-start.19
  553.8 5.0 copy-start.6
  553.8 5.0 copy-start.16
  553.8 5.0 copy-start.48
  553.8 5.0 copy-start.50
  553.8 5.0 copy-start.52
  559.0 7.3 copy-start.9
  559.0 8.8 copy-start.32
  611.3 7.2 copy-start.9
  611.3 8.6 copy-start.32
  673.9 9.6 copy-start.36
  673.9 9.6 copy-start.37
  694.5 6.5 copy-start.41
  700.9 229.9 %reduce-scatter.24.cloned.1.call-start = ((), (), s32[]{:S(2)}) async-start(), calls=%async_computation.20 | async-start | bytes 2359296 | tf_op jit(solution)/shard_map/reduce_scatter | solution.py:250
  706.4 6.3 copy-start.45
  712.7 264.2 %reduce-scatter.22.cloned.1.call-start = ((), (), s32[]{:S(2)}) async-start(), calls=%async_computation.19 | async-start | bytes 5242880 | tf_op jit(solution)/shard_map/reduce_scatter | solution.py:239
  720.2 6.9 copy-start.39
  720.2 6.9 copy-start.43
  745.9 323.4 %reduce-scatter.32.cloned.1.call-start = ((), (), s32[]{:S(2)}) async-start(), calls=%async_computation.24 | async-start | bytes 4718592 | tf_op jit(solution)/shard_map/reduce_scatter | solution.py:262
  755.3 405.4 %reduce-scatter.28.cloned.1.call-start = ((), (), s32[]{:S(2)}) async-start(), calls=%async_computation.22 | async-start | bytes 4718592 | tf_op jit(solution)/shard_map/reduce_scatter | solution.py:256
  765.1 487.2 %reduce-scatter.30.cloned.1.call-start = ((), (), s32[]{:S(2)}) async-start(), calls=%async_computation.23 | async-start | bytes 4718592 | tf_op jit(solution)/shard_map/reduce_scatter | solution.py:259
  775.0 201.9 %copy-start.13 = (bf16[256,2048]{1,0:T(8,128)(2,1)S(1)}, bf16[256,2048]{1,0:T(8,128)(2,1)}, u32[]{:S(2)}) copy-start(bf16[256,2048]{1,0:T(8,128)(2,1)} %param.19) | copy-start | bytes 3145732
  775.0 201.9 %copy-start.53 = (f32[2048]{0:T(1024)S(1)}, f32[2048]{0:T(1024)}, u32[]{:S(2)}) copy-start(f32[2048]{0:T(1024)} %param.21) | copy-start | bytes 24580
  775.0 201.9 %copy-start.60 = (f32[256]{0:T(256)S(1)}, f32[256]{0:T(256)}, u32[]{:S(2)}) copy-start(f32[256]{0:T(256)} %copy-done.59) | copy-start | bytes 3076
  775.0 203.7 %copy-start.68 = (f32[256]{0:T(256)S(1)}, f32[256]{0:T(256)}, u32[]{:S(2)}) copy-start(f32[256]{0:T(256)} %copy-done.67) | copy-start | bytes 3076
  775.0 203.7 %copy-start.64 = (f32[256]{0:T(256)S(1)}, f32[256]{0:T(256)}, u32[]{:S(2)}) copy-start(f32[256]{0:T(256)} %copy-done.63) | copy-start | bytes 3076
  775.0 615.5 %reduce-scatter.40.cloned.1.call-start = ((), (), s32[]{:S(2)}) async-start(), calls=%async_computation.28 | async-start | bytes 1081344
  777.5 203.5 %copy-start.61 = (f32[2048]{0:T(1024)S(1)}, f32[2048]{0:T(1024)}, u32[]{:S(2)}) copy-start(f32[2048]{0:T(1024)} %get-tuple-element.855) | copy-start | bytes 24580
  777.5 203.5 %copy-start.62 = (f32[2048]{0:T(1024)S(1)}, f32[2048]{0:T(1024)}, u32[]{:S(2)}) copy-start(f32[2048]{0:T(1024)} %get-tuple-element.860) | copy-start | bytes 24580
  789.9 192.6 %copy-start.66 = (f32[256]{0:T(256)S(1)}, f32[256]{0:T(256)}, u32[]{:S(2)}) copy-start(f32[256]{0:T(256)} %copy-done.65) | copy-start | bytes 3076
  789.9 192.6 %copy-start.70 = (f32[256]{0:T(256)S(1)}, f32[256]{0:T(256)}, u32[]{:S(2)}) copy-start(f32[256]{0:T(256)} %copy-done.69) | copy-start | bytes 3076
  (49 other events, 132.9 us)
Sparse Core Ops, SparseCore 0:
  14.5 37.1 all-gather.3
  196.2 44.5 reduce-scatter.15
  242.9 53.5 all-gather.5
  379.4 44.5 reduce-scatter.19
  426.4 44.5 reduce-scatter.17
  477.7 34.4 all-gather.7
  515.8 88.2 reduce-scatter.35
  607.8 87.9 reduce-scatter.33
  699.4 88.2 reduce-scatter.37
  791.2 67.9 reduce-scatter.25
  863.2 67.5 reduce-scatter.23
  933.2 43.6 reduce-scatter.21
  980.5 88.6 reduce-scatter.31
  1072.8 87.9 reduce-scatter.27
  1164.2 87.9 reduce-scatter.29
  1254.3 136.1 reduce-scatter.39
